TPU v7x, 32 devices: a whole 2x2x4 slice. The times are simulated.
32 devices in a mesh: slab: 16 (over z, y, core), sub: 2 (over x).
Axes of the slice: x: 2, y: 2, z: 4, core: 2. Of those that a mesh axis runs over, the one named last changes fastest.
Arguments:
- modes: float32 [16, 2, 3, 16, 2048], P('slab', 'sub'), may hold values from -1.8 to 1.8
- connect: int32 [16, 2, 27, 256], P('slab', 'sub'), may hold values from 0 to 2559, as said below
- ghosts: int32 [16, 2, 512], P('slab', 'sub'), may hold values from 0 to 4607, as said below
- inv_jacobian: float32 [16, 2, 3, 3, 27, 256], P('slab', 'sub'), may hold values from -1.05 to 3, as said below
- young: float32 [16, 2, 256], P('slab', 'sub'), may hold values from 0.5 to 2
- density: float32 [16, 2, 256], P('slab', 'sub'), may hold values from 0.5 to 2
- ffd_cell: int32 [16, 2, 3, 2048], P('slab', 'sub'), may hold values from 0 to 4
- ffd_param: float32 [16, 2, 3, 2048], P('slab', 'sub'), may hold values from 0 to 1
- eigen: float32 [16], replicated, may hold values from 4 to 16
Outputs:
- freq_grad: float32 [3, 16, 4096], P(None, 'sub', 'slab')
Inputs may be any that keep to these rules, and one draw needn't show every extreme that they name: `connect`: slots 0 to 2047 are owned, the rest ghost slots; the first 128 elements of every device name owned slots only. `ghosts`: entry (3 a + b) * 512 + n names owned node n < 512 of device ((s + a - 1) mod 16, r + b - 1), never (a, b) = (1, 1), and r + b - 1 always lies in 0 to 1. `inv_jacobian`: every 3 x 3 block has a positive determinant.
All inputs are finite; a program needn't handle non-finite values.
Results may differ from a plain program's by a relative error of at most 0.0003.
Values sent between devices are 32-bit elements; how exact they have to be, the bound alone decides.
No kernel may reach another device: no remote copies, remote signals or barrier semaphores. Data moves between devices by JAX's collectives and lax.ppermute only.
A program may use at most 64 MiB of HBM per device.

v0:
```python
import math

import jax
import jax.numpy as jnp
import numpy as np
from jax import lax
from jax.sharding import PartitionSpec as P

CTRL = 16


def with_halo(block, sides, width, periodic):
    for axis, dim in sides:
        count = lax.axis_size(axis)
        forward = [(i, i + 1) for i in range(count - 1)]
        if periodic:
            forward.append((count - 1, 0))
        backward = [(target, source) for source, target in forward]
        low = lax.ppermute(
            lax.slice_in_dim(block, block.shape[dim] - width, None, axis=dim), axis, forward
        )
        high = lax.ppermute(lax.slice_in_dim(block, 0, width, axis=dim), axis, backward)
        block = jnp.concatenate([low, block, high], axis=dim)
    return block


def triple_product(first, second, third):
    table = (
        first[:, None, None, :, None, None]
        * second[None, :, None, None, :, None]
        * third[None, None, :, None, None, :]
    )
    return table.reshape(27, 27)


def lagrange_tables():
    points = np.array([-math.sqrt(0.6), 0.0, math.sqrt(0.6)])
    gauss_weights = np.array([5.0 / 9.0, 8.0 / 9.0, 5.0 / 9.0])
    basis = np.stack(
        [points * (points - 1.0) / 2.0, 1.0 - points * points, points * (points + 1.0) / 2.0],
        axis=1,
    )
    slopes = np.stack([points - 0.5, -2.0 * points, points + 0.5], axis=1)
    shape_fn = triple_product(basis, basis, basis)
    grad_x = triple_product(slopes, basis, basis)
    grad_y = triple_product(basis, slopes, basis)
    grad_z = triple_product(basis, basis, slopes)
    gradients = np.concatenate([grad_x, grad_y, grad_z], axis=0)
    quad_weights = (
        gauss_weights[:, None, None] * gauss_weights[None, :, None] * gauss_weights[None, None, :]
    ).reshape(27)
    return (shape_fn, gradients, quad_weights)


def element_block(values, inv_jac, young_e, density_e, eigen):
    shape_np, grads_np, weights_np = lagrange_tables()
    shape_fn = jnp.asarray(shape_np, jnp.float32)
    gradients = jnp.asarray(grads_np, jnp.float32)
    quad_weights = jnp.asarray(weights_np, jnp.float32)
    highest = lax.Precision.HIGHEST
    modes_n = eigen.shape[0]
    elems = values.shape[2]
    ref_grad = jnp.einsum("xa,zae->xze", gradients, values, precision=highest).reshape(
        3, 27, 3, modes_n, elems
    )
    at_points = jnp.einsum("qa,zae->qze", shape_fn, values, precision=highest).reshape(
        27, 3, modes_n, elems
    )
    jac = [[inv_jac[ref_dir, comp_b][:, None, :] for comp_b in range(3)] for ref_dir in range(3)]
    disp = [
        [
            ref_grad[0][:, comp_a] * jac[0][comp_b]
            + ref_grad[1][:, comp_a] * jac[1][comp_b]
            + ref_grad[2][:, comp_a] * jac[2][comp_b]
            for comp_b in range(3)
        ]
        for comp_a in range(3)
    ]
    trace_h = disp[0][0] + disp[1][1] + disp[2][2]
    lame = 0.3 / 0.52 * young_e[None, None, :]
    shear = young_e[None, None, :] / 2.6
    stress = [
        [
            shear * (disp[comp_a][comp_b] + disp[comp_b][comp_a])
            + (lame * trace_h if comp_a == comp_b else 0.0)
            for comp_b in range(3)
        ]
        for comp_a in range(3)
    ]
    energy = 0.5 * sum(
        (
            stress[comp_a][comp_b] * disp[comp_a][comp_b]
            for comp_a in range(3)
            for comp_b in range(3)
        )
    )
    kinetic = at_points[:, 0] ** 2 + at_points[:, 1] ** 2 + at_points[:, 2] ** 2
    iso_part = 2.0 * energy - eigen[None, :, None] * density_e[None, None, :] * kinetic
    eshelby = [
        [
            (iso_part if comp_a == comp_b else 0.0)
            - 2.0
            * (
                disp[0][comp_a] * stress[0][comp_b]
                + disp[1][comp_a] * stress[1][comp_b]
                + disp[2][comp_a] * stress[2][comp_b]
            )
            for comp_b in range(3)
        ]
        for comp_a in range(3)
    ]
    determinant = (
        inv_jac[0, 0] * (inv_jac[1, 1] * inv_jac[2, 2] - inv_jac[1, 2] * inv_jac[2, 1])
        - inv_jac[0, 1] * (inv_jac[1, 0] * inv_jac[2, 2] - inv_jac[1, 2] * inv_jac[2, 0])
        + inv_jac[0, 2] * (inv_jac[1, 0] * inv_jac[2, 1] - inv_jac[1, 1] * inv_jac[2, 0])
    )
    factor = (quad_weights[:, None] / determinant)[:, None, :]
    proj = [
        [
            factor
            * (
                eshelby[comp_a][0] * jac[ref_dir][0]
                + eshelby[comp_a][1] * jac[ref_dir][1]
                + eshelby[comp_a][2] * jac[ref_dir][2]
            )
            for comp_a in range(3)
        ]
        for ref_dir in range(3)
    ]
    stacked = jnp.stack([jnp.stack(proj[ref_dir], axis=1) for ref_dir in range(3)], axis=0)
    stacked = stacked.reshape(81, 3 * modes_n, elems)
    return jnp.einsum("xb,xze->zbe", gradients, stacked, precision=highest)


def bernstein(cells, params, count):
    offset = jnp.arange(count, dtype=jnp.int32)[:, None] - 3 * cells[None, :]
    param = params[None, :]
    other = 1.0 - param
    return (
        jnp.where(offset == 0, other**3, 0.0)
        + jnp.where(offset == 1, 3.0 * param * other**2, 0.0)
        + jnp.where(offset == 2, 3.0 * param**2 * other, 0.0)
        + jnp.where(offset == 3, param**3, 0.0)
    )


def contract(grads, cells, params, ctrl):
    channels, nodes = grads.shape
    width = math.gcd(nodes, 512)
    count = nodes // width

    def contract_step(total, inputs):
        piece, cell_b, param_b = inputs
        along_x = bernstein(cell_b[0], param_b[0], ctrl)
        along_y = bernstein(cell_b[1], param_b[1], ctrl)
        along_z = bernstein(cell_b[2], param_b[2], ctrl)
        left = (piece[:, None, :] * along_x[None, :, :]).reshape(channels * ctrl, width)
        right = (along_y[:, None, :] * along_z[None, :, :]).reshape(ctrl * ctrl, width)
        return (
            total
            + lax.dot_general(
                left, right, (((1,), (1,)), ((), ())), precision=lax.Precision.HIGHEST
            ),
            None,
        )

    pieces = grads.reshape(channels, count, width).transpose(1, 0, 2)
    cell_blocks = cells.reshape(3, count, width).transpose(1, 0, 2)
    param_blocks = params.reshape(3, count, width).transpose(1, 0, 2)
    total, _ = lax.scan(
        contract_step,
        jnp.zeros((channels * ctrl, ctrl * ctrl), jnp.float32),
        (pieces, cell_blocks, param_blocks),
    )
    return total.reshape(3, channels // 3, ctrl**3)


def assemble(slot_vals, connect, inv_jacobian, young, density, eigen):
    channels, slots = slot_vals.shape
    nodes_el = connect.shape[2]
    elems = connect.shape[3]
    width = math.gcd(elems, 128)
    count = elems // width
    conn_blocks = connect.reshape(nodes_el, count, width).transpose(1, 0, 2)
    jac_blocks = inv_jacobian.reshape(3, 3, inv_jacobian.shape[4], count, width).transpose(
        3, 0, 1, 2, 4
    )
    young_blocks = young.reshape(count, width)
    density_blocks = density.reshape(count, width)

    def assemble_step(grad_acc, inputs):
        columns, jac_b, young_b, density_b = inputs
        contrib = element_block(slot_vals[:, columns], jac_b, young_b, density_b, eigen)
        return (grad_acc.at[:, columns].add(contrib), None)

    start = jnp.zeros((channels, slots), jnp.float32)
    grad_acc, _ = lax.scan(
        assemble_step, start, (conn_blocks, jac_blocks, young_blocks, density_blocks)
    )
    return grad_acc


def on_device(modes, connect, ghosts, inv_jacobian, young, density, ffd_cell, ffd_param, eigen):
    channels = modes.shape[2] * modes.shape[3]
    nown = modes.shape[4]
    iface = nown // 4
    own_vals = modes.reshape(channels, nown)
    own_cells = ffd_cell.reshape(3, nown)
    own_params = ffd_param.reshape(3, nown)
    payload = jnp.concatenate(
        [own_vals[:, :iface], own_cells[:, :iface].astype(jnp.float32), own_params[:, :iface]],
        axis=0,
    )
    rows_out = payload.shape[0]
    cycle_part = with_halo(payload[None, None], (("slab", 0),), 1, True)
    beside_all = with_halo(cycle_part, (("sub", 1),), 1, False)
    neighbour = beside_all.reshape(9, rows_out, iface)
    ghost_list = ghosts.reshape(-1)
    block_id = ghost_list // iface
    node_at = ghost_list % iface
    ghost_rows = neighbour[block_id, :, node_at].T
    slot_vals = jnp.concatenate([own_vals, ghost_rows[:channels]], axis=1)
    slot_grad = assemble(
        slot_vals, connect, inv_jacobian, young.reshape(-1), density.reshape(-1), eigen
    )
    slot_cells = jnp.concatenate(
        [own_cells, ghost_rows[channels : channels + 3].astype(jnp.int32)], axis=1
    )
    slot_params = jnp.concatenate([own_params, ghost_rows[channels + 3 : channels + 6]], axis=1)
    design = contract(slot_grad, slot_cells, slot_params, CTRL)
    design = design * (0.5 / jnp.sqrt(eigen))[None, :, None]
    by_cycle = lax.psum_scatter(design, "slab", scatter_dimension=2, tiled=True)
    result = lax.psum_scatter(by_cycle, "sub", scatter_dimension=1, tiled=True)
    return result


def solution(mesh):
    return jax.shard_map(
        on_device,
        mesh=mesh,
        in_specs=(
            P("slab", "sub", None, None, None),
            P("slab", "sub", None, None),
            P("slab", "sub", None),
            P("slab", "sub", None, None, None, None),
            P("slab", "sub", None),
            P("slab", "sub", None),
            P("slab", "sub", None, None),
            P("slab", "sub", None, None),
            P(),
        ),
        out_specs=P(None, "sub", "slab"),
        check_vma=False,
    )
```

profile of v0, /device:TPU:0, one launch (start us, length us, event | category | flops | bytes accessed | tf_op | source)
XLA Modules:
  0.0 224.0 jit_solution(3928767350223652878)
XLA Ops:
  6.5 0.9 slice.343
  7.4 0.8 copy.146
  8.2 0.8 copy.147
  9.0 0.5 collective-permute-start
  9.5 5.0 %collective-permute-start.1 = (f32[1,1,54,512]{3,2,1,0:T(8,128)S(1)}, f32[1,1,54,512]{3,2,1,0:T(8,128)S(1)}, u32[]{:S(2)}, u32[]{:S(2)}) collective-permute-start(f32[1,1,54,512]{3,2,1,0:T(8,128)S(1)} %maximum_bitcast_fusion.3), channel_id=1, source_target_pairs={{2,0},{4,2},{6,4},{8,6},{10,8},{12,10},{14,12},{16,14},{18,16},{20... | collective-permute-start | bytes 331784 | tf_op jit(solution)/shard_map/ppermute | solution.py:22
  14.6 2.5 %collective-permute-done = f32[1,1,54,512]{3,2,1,0:T(8,128)S(1)} collective-permute-done((f32[1,1,54,512]{3,2,1,0:T(8,128)S(1)}, f32[1,1,54,512]{3,2,1,0:T(8,128)S(1)}, u32[]{:S(2)}, u32[]{:S(2)}) %collective-permute-start) | collective-permute-done | bytes 110624 | tf_op jit(solution)/shard_map/ppermute | solution.py:19
  17.1 3.9 %collective-permute-start.2 = (f32[3,1,54,512]{3,2,1,0:T(8,128)S(1)}, f32[3,1,54,512]{3,2,1,0:T(8,128)S(1)}, u32[]{:S(2)}, u32[]{:S(2)}) collective-permute-start(f32[3,1,54,512]{3,2,1,0:T(8,128)S(1)} %pad_maximum_fusion.3), channel_id=1, source_target_pairs={{0,1},{2,3},{4,5},{6,7},{8,9},{10,11},{12,13},{14,15},{16,17},{18,... | collective-permute-start | bytes 995336 | tf_op jit(solution)/shard_map/ppermute | solution.py:19
  21.0 1.3 collective-permute-start.3
  22.3 1.2 rsqrt_multiply_fusion
  23.5 0.7 fusion.36
  24.2 4.3 %collective-permute-done.2 = f32[3,1,54,512]{3,2,1,0:T(8,128)S(1)} collective-permute-done((f32[3,1,54,512]{3,2,1,0:T(8,128)S(1)}, f32[3,1,54,512]{3,2,1,0:T(8,128)S(1)}, u32[]{:S(2)}, u32[]{:S(2)}) %collective-permute-start.2) | collective-permute-done | bytes 331808 | tf_op jit(solution)/shard_map/ppermute | solution.py:19
  28.5 4.1 %collective-permute-done.3 = f32[3,1,54,512]{3,2,1,0:T(8,128)S(1)} collective-permute-done((f32[3,1,54,512]{3,2,1,0:T(8,128)S(1)}, f32[3,1,54,512]{3,2,1,0:T(8,128)S(1)}, u32[]{:S(2)}, u32[]{:S(2)}) %collective-permute-start.3) | collective-permute-done | bytes 331808 | tf_op jit(solution)/shard_map/ppermute | solution.py:22
  32.7 0.9 copy.34
  33.6 3.7 %gather_fusion.1 = f32[512,54]{1,0:T(8,128)S(1)} fusion(f32[9,54,512]{1,2,0:T(8,128)S(1)} %bitcast.243, s32[512]{0:T(512)S(1)} %bitcast.240), kind=kCustom, calls=%fused_computation.1 | custom fusion | bytes 225280 | tf_op jit(solution)/shard_map/gather | solution.py:221
  37.7 0.6 reshape.855
  38.4 0.6 reshape.856
  40.0 84.8 %while.24 = (s32[]{:T(128)}, f32[48,2560]{0,1:T(8,128)S(1)}, s32[2,27,128]{2,0,1:T(2,128)S(1)}, f32[2,3,3,27,128]{4,0,3,2,1:T(2,128)}, f32[2,128]{1,0:T(2,128)S(...) while((s32[]{:T(128)}, f32[48,2560]{0,1:T(8,128)S(1)}, ...), condition=%wide.region_2.3_spmd.clone, body=%wide.region_0.2_spmd.sunk.clone.sunk | while | flops 390568960 | bytes 46023428 | solution.py:197
  40.3 7.4 %gather_fusion = f32[3456,48]{1,0:T(8,128)} fusion(f32[48,2560]{0,1:T(8,128)S(1)} %get-tuple-element.609, s32[4096]{0:T(1024)S(1)} %pad_clamp_fusion.2), kind=kCustom, calls=%fused_computation.clone.1 | custom fusion | bytes 1340928 | tf_op jit(solution)/shard_map/while/body/eval_jaxpr/gather | solution.py:193
  47.6 2.3 %copy.162 = f32[27,128,48]{1,0,2:T(8,128)S(1)} copy(f32[27,128,48]{2,1,0:T(8,128)} %bitcast.234) | data formatting | bytes 1327104 | tf_op jit(solution)/shard_map/while/body/eval_jaxpr/gather | solution.py:193
  49.9 1.9 fusion.74
  52.3 0.8 fusion.76
  53.3 0.8 copy-done.2
  54.2 0.5 multiply_add_fusion.19
  54.9 2.0 add_multiply_fusion.16
  56.9 0.6 add_multiply_fusion.17
  58.1 2.0 fusion.79
  60.1 1.8 copy.163
  61.9 20.5 %scatter_fusion = f32[48,2560]{0,1:T(8,128)S(1)} fusion(f32[48,2560]{0,1:T(8,128)S(1)} %get-tuple-element.593, s32[3456]{0:T(1024)S(1)} %fusion.73, f32[3456,48]{1,0:T(8,128)} %bitcast.231), kind=kCustom, calls=%fused_computation.2.clone.1 | custom fusion | flops 165888 | bytes 2004480 | tf_op jit(solution)/shard_map/while/body/eval_jaxpr/scatter-add | solution.py:194
  82.5 7.4 %gather_fusion = f32[3456,48]{1,0:T(8,128)} fusion(f32[48,2560]{0,1:T(8,128)S(1)} %get-tuple-element.609, s32[4096]{0:T(1024)S(1)} %pad_clamp_fusion.2), kind=kCustom, calls=%fused_computation.clone.1 | custom fusion | bytes 1340928 | tf_op jit(solution)/shard_map/while/body/eval_jaxpr/gather | solution.py:193
  89.9 2.3 %copy.162 = f32[27,128,48]{1,0,2:T(8,128)S(1)} copy(f32[27,128,48]{2,1,0:T(8,128)} %bitcast.234) | data formatting | bytes 1327104 | tf_op jit(solution)/shard_map/while/body/eval_jaxpr/gather | solution.py:193
  92.1 1.9 fusion.74
  94.5 0.8 fusion.76
  95.5 0.8 copy-done.2
  96.4 0.5 multiply_add_fusion.19
  97.1 2.0 add_multiply_fusion.16
  99.1 0.6 add_multiply_fusion.17
  100.3 2.0 fusion.79
  102.3 1.8 copy.163
  104.1 20.5 %scatter_fusion = f32[48,2560]{0,1:T(8,128)S(1)} fusion(f32[48,2560]{0,1:T(8,128)S(1)} %get-tuple-element.593, s32[3456]{0:T(1024)S(1)} %fusion.73, f32[3456,48]{1,0:T(8,128)} %bitcast.231), kind=kCustom, calls=%fused_computation.2.clone.1 | custom fusion | flops 165888 | bytes 2004480 | tf_op jit(solution)/shard_map/while/body/eval_jaxpr/scatter-add | solution.py:194
  124.9 1.2 copy.42
  126.1 23.2 %while.25 = (s32[]{:T(128)}, f32[768,256]{1,0:T(8,128)S(1)}, f32[5,48,512]{2,1,0:T(8,128)}, s32[5,3,512]{2,0,1:T(8,128)}, f32[5,3,512]{2,0,1:T(8,128)}, /*index=5*/s32[]{:T(128)}, s32[]{:T(128)}, s32[]{}, s32[]{}) while((s32[]{:T(128)}, f32[768,256]{1,0:T(8,128)S(1)}, f32[5,48,512]{2,1,0:T(8,128)}, s32[5,3,512]{2,0,1:T(8,128)}, ...), condition=%wide.region_4.5_spmd.clone, body=%wide.region_3.4_spmd.clone.sunk | while | flops 1209187328 | bytes 6344859 | solution.py:170
  126.1 0.8 constant_dynamic-slice_fusion.12
  126.8 0.8 fusion.82
  127.6 0.9 dynamic-slice_bitcast_fusion.5
  128.9 1.8 convolution_add_fusion.2
  130.7 0.8 constant_dynamic-slice_fusion.12
  131.5 0.8 fusion.82
  132.3 0.9 dynamic-slice_bitcast_fusion.5
  133.5 1.8 convolution_add_fusion.2
  135.4 0.8 constant_dynamic-slice_fusion.12
  136.1 0.8 fusion.82
  136.9 0.9 dynamic-slice_bitcast_fusion.5
  138.2 1.8 convolution_add_fusion.2
  140.0 0.8 constant_dynamic-slice_fusion.12
  140.8 0.8 fusion.82
  141.6 0.9 dynamic-slice_bitcast_fusion.5
  142.8 1.8 convolution_add_fusion.2
  144.6 0.8 constant_dynamic-slice_fusion.12
  145.4 0.8 fusion.82
  146.2 0.9 dynamic-slice_bitcast_fusion.5
  147.5 1.8 convolution_add_fusion.2
  149.4 1.0 broadcast_multiply_fusion.3
  150.5 55.3 %reduce-scatter.3.cloned.1.call-done = f32[3,16,256]{2,1,0:T(8,128)} async-done(((f32[3,16,4096]{2,1,0:T(8,128)}), f32[3,16,256]{2,1,0:T(8,128)}) %reduce-scatter.3.cloned.1.call-update) | async-done | bytes 49168 | tf_op jit(solution)/shard_map/reduce_scatter | solution.py:232
  205.9 11.2 %reduce-scatter.5.cloned.1.call-done = f32[3,8,256]{2,1,0:T(8,128)} async-done(((f32[3,16,256]{2,1,0:T(8,128)}), f32[3,8,256]{2,1,0:T(8,128)}) %reduce-scatter.5.cloned.1.call-update) | async-done | bytes 24592 | tf_op jit(solution)/shard_map/reduce_scatter | solution.py:233
  (113 shorter events, 6.4 us)
Async XLA Ops:
  6.5 199.3 %reduce-scatter.3.cloned.1.call-start = ((), (), s32[]{:S(2)}) async-start(), calls=%async_computation.2 | async-start | bytes 835584 | tf_op jit(solution)/shard_map/reduce_scatter | solution.py:232
  9.0 8.1 %collective-permute-start = (f32[1,1,54,512]{3,2,1,0:T(8,128)S(1)}, f32[1,1,54,512]{3,2,1,0:T(8,128)S(1)}, u32[]{:S(2)}, u32[]{:S(2)}) collective-permute-start(f32[1,1,54,512]{3,2,1,0:T(8,128)S(1)} %maximum_bitcast_fusion.3), channel_id=1, source_target_pairs={{0,2},{2,4},{4,6},{6,8},{8,10},{10,12},{12,14},{14,16},{16,18},{18... | collective-permute-start | bytes 331784 | tf_op jit(solution)/shard_map/ppermute | solution.py:19
  9.5 7.6 %collective-permute-start.1 = (f32[1,1,54,512]{3,2,1,0:T(8,128)S(1)}, f32[1,1,54,512]{3,2,1,0:T(8,128)S(1)}, u32[]{:S(2)}, u32[]{:S(2)}) collective-permute-start(f32[1,1,54,512]{3,2,1,0:T(8,128)S(1)} %maximum_bitcast_fusion.3), channel_id=1, source_target_pairs={{2,0},{4,2},{6,4},{8,6},{10,8},{12,10},{14,12},{16,14},{18,16},{20... | collective-permute-start | bytes 331784 | tf_op jit(solution)/shard_map/ppermute | solution.py:22
  17.1 11.4 %collective-permute-start.2 = (f32[3,1,54,512]{3,2,1,0:T(8,128)S(1)}, f32[3,1,54,512]{3,2,1,0:T(8,128)S(1)}, u32[]{:S(2)}, u32[]{:S(2)}) collective-permute-start(f32[3,1,54,512]{3,2,1,0:T(8,128)S(1)} %pad_maximum_fusion.3), channel_id=1, source_target_pairs={{0,1},{2,3},{4,5},{6,7},{8,9},{10,11},{12,13},{14,15},{16,17},{18,... | collective-permute-start | bytes 995336 | tf_op jit(solution)/shard_map/ppermute | solution.py:19
  21.0 11.6 %collective-permute-start.3 = (f32[3,1,54,512]{3,2,1,0:T(8,128)S(1)}, f32[3,1,54,512]{3,2,1,0:T(8,128)S(1)}, u32[]{:S(2)}, u32[]{:S(2)}) collective-permute-start(f32[3,1,54,512]{3,2,1,0:T(8,128)S(1)} %pad_maximum_fusion.3), channel_id=1, source_target_pairs={{1,0},{3,2},{5,4},{7,6},{9,8},{11,10},{13,12},{15,14},{17,16},{19,... | collective-permute-start | bytes 995336 | tf_op jit(solution)/shard_map/ppermute | solution.py:22
  37.3 1.9 copy-start.3
  39.2 0.7 copy-start.1
  39.3 0.7 copy-start.4
  39.3 0.8 copy-start.5
  39.3 0.7 copy-start.6
  39.3 0.7 copy-start.7
  39.3 0.7 copy-start.8
  39.3 0.7 copy-start.9
  53.1 0.9 copy-start.2
  95.3 0.9 copy-start.2
  124.9 1.2 copy-start
  126.1 23.4 %copy-start.10 = (f32[16]{0:T(128)S(1)}, f32[16]{0:T(128)}, u32[]{:S(2)}) copy-start(f32[16]{0:T(128)} %rsqrt_multiply_fusion) | copy-start | bytes 196
  150.5 66.6 %reduce-scatter.5.cloned.1.call-start = ((), (), s32[]{:S(2)}) async-start(), calls=%async_computation.3 | async-start | bytes 73728 | tf_op jit(solution)/shard_map/reduce_scatter | solution.py:233
Sparse Core Ops, SparseCore 0:
  150.6 55.2 reduce-scatter.2
  208.1 9.0 reduce-scatter.4
where the time goes:
time: 226 us; the launch traced here: 224 us
  waiting for transfers between devices  77.6 us (34%)
  other arithmetic  57.3 us (25%)
  local copies, waits for them, and re-layouts  45.2 us (20%)
  matrix products  18.4 us (8%)
  between operations  13.6 us (6%)
  starting transfers between devices  10.8 us (5%)
    reduce_scatter x1, waiting for transfers between devices, on_device(): by_cycle = lax.psum_scatter(design, 'slab', scatter_dimension=2, tiled=True)  55.3 us
    scatter-add x2, other arithmetic, assemble_step(): return (grad_acc.at[:, columns].add(contrib), None)  41 us
    gather x4, local copies, waits for them, and re-layouts, assemble_step(): slot_vals[:, columns]  19.3 us
    reduce_scatter x1, waiting for transfers between devices, on_device(): result = lax.psum_scatter(by_cycle, 'sub', scatter_dimension=1, tiled=True)  11.2 us
    dot_general x5, matrix products, contract_step(): lax.dot_general(left, right, (((1,), (1,)), ((), ())), precision=lax.Prec...  9.07 us
    ppermute x2, waiting for transfers between devices, with_halo(): lax.ppermute(lax.slice_in_dim(block, block.shape[dim] - width, None, axis...  6.82 us
    ppermute x2, starting transfers between devices, with_halo(): lax.ppermute(lax.slice_in_dim(block, 0, width, axis=dim), axis, backward)  6.34 us
    mul x6, other arithmetic, element_block(): factor * (eshelby[comp_a][0] * jac[ref_dir][0] + eshelby[comp_a][1] * jac...  5.77 us
  transfers between devices with their start and end apart: 6, of which 5 were waited for; matrix products, arithmetic and copies ran while one was open for 1% of the time, Pallas kernels for 0%

commit v1 on v0

v1 whole, which is shorter than its diff:
```python
import math

import jax
import jax.numpy as jnp
from jax import lax
from jax.experimental import pallas as pl
from jax.experimental.pallas import tpu as pltpu
from jax.sharding import PartitionSpec as P

CTRL = 16
LANES = 128
ROWS = 56
GROUP = 8
ROOT = math.sqrt(0.6)
HALF_ROOT = 0.5 * ROOT
GAUSS = (5.0 / 9.0, 8.0 / 9.0, 5.0 / 9.0)


def interp(low, mid, high):
    even = 0.3 * (low + high) + 0.4 * mid
    odd = HALF_ROOT * (high - low)
    return even - odd, mid, even + odd


def slope(low, mid, high):
    odd = 0.5 * (high - low)
    even = ROOT * (low + high - 2.0 * mid)
    return odd - even, odd, odd + even


def interp_t(low, mid, high):
    total = low + high
    even = 0.3 * total
    odd = HALF_ROOT * (high - low)
    return even - odd, 0.4 * total + mid, even + odd


def slope_t(low, mid, high):
    odd = 0.5 * (low + mid + high)
    even = ROOT * (high - low)
    return even - odd, -2.0 * even, even + odd


def along(axis, fn, grid):
    out = [None] * 27
    step = (9, 3, 1)[axis]
    for start in range(27):
        if (start // step) % 3 == 0:
            line = fn(grid[start], grid[start + step], grid[start + 2 * step])
            for pos in range(3):
                out[start + pos * step] = line[pos]
    return out


def split_pair(value):
    high = value.astype(jnp.bfloat16)
    low = (value - high.astype(jnp.float32)).astype(jnp.bfloat16)
    return high, low


def fill_rows(tab, col, width, modes_k, cells, params):
    comps = len(modes_k)
    modes_n = modes_k[0].shape[0]
    for comp, block in enumerate(modes_k):
        tab[pl.ds(comp * modes_n, modes_n), pl.ds(col, width)] = block
    base = comps * modes_n
    tab[pl.ds(base, 8), pl.ds(col, width)] = jnp.concatenate(
        [cells.astype(jnp.float32), params, jnp.zeros((2, width), jnp.float32)], axis=0
    )


def pack_kernel(modes, cells, params, out):
    width = out.shape[1]
    fill_rows(
        out,
        0,
        width,
        [modes[0, 0, comp, :, :width] for comp in range(3)],
        cells[0, 0, :, :width],
        params[0, 0, :, :width],
    )


def one_hot(index_row, depth, iota):
    width = index_row.shape[1]
    wide = jnp.broadcast_to(index_row, (16, width))
    upper = wide >> 8
    lower = (wide & 255).astype(jnp.float32)
    parts = []
    for chunk in range(depth // 256):
        code = jnp.where(upper == chunk, lower, -1.0).astype(jnp.bfloat16)
        hit = iota.reshape(16, 16, width) == code[None]
        parts.append(
            jnp.where(hit, jnp.bfloat16(1), jnp.bfloat16(0)).reshape(256, width)
        )
    return jnp.concatenate(parts, axis=0)


def bernstein(cell, param, count):
    offset = lax.broadcasted_iota(jnp.int32, (count, LANES), 0) - jnp.broadcast_to(
        3 * cell.astype(jnp.int32), (count, LANES)
    )
    other = 1.0 - param
    square = param * param
    other_square = other * other
    result = jnp.zeros((count, LANES), jnp.float32)
    for which, poly in enumerate(
        (other_square * other, 3.0 * param * other_square, 3.0 * square * other, square * param)
    ):
        result = jnp.where(offset == which, jnp.broadcast_to(poly, (count, LANES)), result)
    return result


def make_kernel(elem_start, nblocks, iface, first):
    def kernel(*refs):
        modes, cells, params, conn, jac, young, density, eigen = refs[:8]
        pos = 8
        if not first:
            ghosts, blocks, acc_in = refs[pos], refs[pos + 1 : pos + 1 + len(nblocks)], refs[
                pos + 1 + len(nblocks)
            ]
            pos += 2 + len(nblocks)
        out = refs[pos]
        tab32, tab, conn_s, iota, vals, field, proj, jac_s, grads = refs[pos + 1 : pos + 10]
        if not first:
            ghost32, ghost_tab = refs[pos + 10 : pos + 12]
        modes_n = modes.shape[3]
        nown = modes.shape[4]
        nodes = conn.shape[2]
        groups = modes_n // GROUP
        lanes = pl.ds(elem_start, LANES)
        fill_rows(
            tab32, 0, nown, [modes[0, 0, comp] for comp in range(3)], cells[0, 0], params[0, 0]
        )
        high, low = split_pair(tab32[...])
        tab[:, pl.ds(0, nown)] = jnp.concatenate([high, low], axis=0)
        iota[...] = lax.broadcasted_iota(jnp.int32, (256, 256), 0).astype(jnp.float32).astype(
            jnp.bfloat16
        )
        depth = nown
        if not first:
            col = 0
            for block, names in zip(blocks, nblocks):
                for name in names:
                    piece = block[...] if name is None else block[name]
                    high, low = split_pair(piece)
                    ghost_tab[:, pl.ds(col, iface)] = jnp.concatenate([high, low], axis=0)
                    col += iface
            nghost = ghosts.shape[2]
            for start in range(0, nghost, 256):
                index = ghosts[0, :, pl.ds(start, 256)]
                picked = jnp.dot(
                    ghost_tab[...],
                    one_hot(index, col, iota[...]),
                    preferred_element_type=jnp.float32,
                )
                tab[:, pl.ds(nown + start, 256)] = picked.astype(jnp.bfloat16)
            depth = nown + nghost
        conn_s[...] = jnp.full(conn_s.shape, -1, jnp.int32)
        conn_s[pl.ds(0, nodes), :] = conn[0, 0, :, lanes]

        def gather(step, carry):
            for inner in range(2):
                node = step * 4 + inner * 2
                index = jnp.concatenate(
                    [conn_s[pl.ds(node, 1), :], conn_s[pl.ds(node + 1, 1), :]], axis=1
                )
                picked = jnp.dot(
                    tab[...],
                    one_hot(index, depth, iota[...]),
                    preferred_element_type=jnp.float32,
                )
                both = picked[:ROWS] + picked[ROWS:]
                vals[node] = both[:, :LANES]
                vals[node + 1] = both[:, LANES:]
            return carry

        lax.fori_loop(0, conn_s.shape[0] // 4, gather, 0)

        inv = [[jac[0, 0, ref_dir, comp, :, lanes] for comp in range(3)] for ref_dir in range(3)]
        det = (
            inv[0][0] * (inv[1][1] * inv[2][2] - inv[1][2] * inv[2][1])
            - inv[0][1] * (inv[1][0] * inv[2][2] - inv[1][2] * inv[2][0])
            + inv[0][2] * (inv[1][0] * inv[2][1] - inv[1][1] * inv[2][0])
        )
        point = lax.broadcasted_iota(jnp.int32, det.shape, 0)
        weight = jnp.ones(det.shape, jnp.float32)
        for digit in (9, 3, 1):
            weight = weight * jnp.where((point // digit) % 3 == 1, GAUSS[1], GAUSS[0])
        factor = 2.0 * weight / det
        for ref_dir in range(3):
            for comp in range(3):
                jac_s[ref_dir * 3 + comp] = inv[ref_dir][comp]
                jac_s[9 + ref_dir * 3 + comp] = inv[ref_dir][comp] * factor
        stiff = young[0, :, lanes]
        lame = jnp.broadcast_to(0.3 / 0.52 * stiff, (GROUP, LANES))
        shear = jnp.broadcast_to(stiff / 2.6, (GROUP, LANES))
        dens = jnp.broadcast_to(density[0, :, lanes], (GROUP, LANES))

        def element(group, carry):
            modes_at = pl.multiple_of(group * GROUP, GROUP)
            eig = jnp.broadcast_to(eigen[pl.ds(modes_at, GROUP), :], (GROUP, LANES))
            inertia = eig * dens
            scale = 0.5 / jnp.sqrt(eig)
            for comp in range(3):
                grid = [
                    vals[node, pl.ds(comp * modes_n + modes_at, GROUP), :] for node in range(27)
                ]
                x_in = along(0, interp, grid)
                x_sl = along(0, slope, grid)
                xy_in = along(1, interp, x_in)
                for which, res in (
                    (0, along(2, interp, along(1, interp, x_sl))),
                    (1, along(2, interp, along(1, slope, x_in))),
                    (2, along(2, slope, xy_in)),
                    (3, along(2, interp, xy_in)),
                ):
                    for q in range(27):
                        field[which, q, comp] = res[q]

            def at_point(q, inner_carry):
                ref = [[field[which, q, comp] for comp in range(3)] for which in range(4)]
                jm = [
                    [
                        jnp.broadcast_to(jac_s[d * 3 + j, pl.ds(q, 1), :], (GROUP, LANES))
                        for j in range(3)
                    ]
                    for d in range(3)
                ]
                js = [
                    [
                        jnp.broadcast_to(jac_s[9 + d * 3 + j, pl.ds(q, 1), :], (GROUP, LANES))
                        for j in range(3)
                    ]
                    for d in range(3)
                ]
                disp = [
                    [
                        ref[0][k] * jm[0][j] + ref[1][k] * jm[1][j] + ref[2][k] * jm[2][j]
                        for j in range(3)
                    ]
                    for k in range(3)
                ]
                trace = lame * (disp[0][0] + disp[1][1] + disp[2][2])
                twice = shear + shear
                diag = [twice * disp[k][k] + trace for k in range(3)]
                sums = {
                    (0, 1): disp[0][1] + disp[1][0],
                    (0, 2): disp[0][2] + disp[2][0],
                    (1, 2): disp[1][2] + disp[2][1],
                }
                off = {pair: shear * value for pair, value in sums.items()}

                def sigma(k, j):
                    return diag[k] if k == j else off[(min(k, j), max(k, j))]

                work = (
                    diag[0] * disp[0][0]
                    + diag[1] * disp[1][1]
                    + diag[2] * disp[2][2]
                    + off[(0, 1)] * sums[(0, 1)]
                    + off[(0, 2)] * sums[(0, 2)]
                    + off[(1, 2)] * sums[(1, 2)]
                )
                kinetic = ref[3][0] * ref[3][0] + ref[3][1] * ref[3][1] + ref[3][2] * ref[3][2]
                iso = 0.5 * (work - inertia * kinetic)
                for d in range(3):
                    tau = [
                        js[d][0] * sigma(k, 0) + js[d][1] * sigma(k, 1) + js[d][2] * sigma(k, 2)
                        for k in range(3)
                    ]
                    for i in range(3):
                        proj[d, q, i] = iso * js[d][i] - (
                            disp[0][i] * tau[0] + disp[1][i] * tau[1] + disp[2][i] * tau[2]
                        )
                return inner_carry

            lax.fori_loop(0, 27, at_point, 0)
            for comp in range(3):
                px = along(1, interp_t, along(2, interp_t, [proj[0, q, comp] for q in range(27)]))
                py = along(1, slope_t, along(2, interp_t, [proj[1, q, comp] for q in range(27)]))
                pz = along(1, interp_t, along(2, slope_t, [proj[2, q, comp] for q in range(27)]))
                from_x = along(0, slope_t, px)
                from_yz = along(0, interp_t, [first_v + second_v for first_v, second_v in zip(py, pz)])
                for node in range(27):
                    grads[
                        node, pl.ds(group * (3 * GROUP) + comp * GROUP, GROUP), :
                    ] = scale * (from_x[node] + from_yz[node])
            return carry

        lax.fori_loop(0, groups, element, 0)
        grads[27] = jnp.zeros((3 * modes_n, LANES), jnp.float32)
        base = 3 * modes_n
        if first:
            out[...] = jnp.zeros(out.shape, jnp.float32)
        else:
            out[...] = acc_in[...]

        def contract(step, carry):
            lefts = []
            rights = []
            for inner in range(2):
                node = step * 2 + inner
                rows = vals[node, pl.ds(base, 8), :]
                along_x, along_y, along_z = [
                    bernstein(rows[dim : dim + 1], rows[3 + dim : 4 + dim], CTRL)
                    for dim in range(3)
                ]
                piece = grads[node]
                left = (along_x[:, None, :] * piece[None, :, :]).reshape(
                    CTRL * 3 * modes_n, LANES
                )
                right = (along_y[:, None, :] * along_z[None, :, :]).reshape(CTRL * CTRL, LANES)
                lefts.append(split_pair(left))
                rights.append(split_pair(right))
            left_all = jnp.concatenate(
                [lefts[0][0], lefts[1][0], lefts[0][0], lefts[1][0], lefts[0][1], lefts[1][1]],
                axis=1,
            )
            right_all = jnp.concatenate(
                [
                    rights[0][0],
                    rights[1][0],
                    rights[0][1],
                    rights[1][1],
                    rights[0][0],
                    rights[1][0],
                ],
                axis=1,
            )
            out[...] += lax.dot_general(
                left_all,
                right_all,
                (((1,), (1,)), ((), ())),
                preferred_element_type=jnp.float32,
            )
            return carry

        lax.fori_loop(0, 14, contract, 0)

    return kernel


def run_elements(elem_start, arrays, halo, acc):
    modes, connect, jac = arrays[0], arrays[3], arrays[4]
    modes_n, nown = modes.shape[3], modes.shape[4]
    channels = 3 * modes_n
    operands = list(arrays)
    nblocks = ()
    iface = 0
    nghost = 0
    extra = []
    if halo is not None:
        ghosts, blocks, nblocks = halo
        iface = blocks[0].shape[-1]
        nghost = ghosts.shape[2]
        operands += [ghosts, *blocks, acc]
        total = sum(len(names) for names in nblocks)
        extra = [
            pltpu.VMEM((8, LANES), jnp.float32),
            pltpu.VMEM((2 * ROWS, total * iface), jnp.bfloat16),
        ]
    f32 = jnp.float32
    scratch = [
        pltpu.VMEM((ROWS, nown), f32),
        pltpu.VMEM((2 * ROWS, nown + nghost), jnp.bfloat16),
        pltpu.VMEM((28, LANES), jnp.int32),
        pltpu.VMEM((256, 256), jnp.bfloat16),
        pltpu.VMEM((28, ROWS, LANES), f32),
        pltpu.VMEM((4, 27, 3, GROUP, LANES), f32),
        pltpu.VMEM((3, 27, 3, GROUP, LANES), f32),
        pltpu.VMEM((18, 27, LANES), f32),
        pltpu.VMEM((28, channels, LANES), f32),
    ] + extra
    return pl.pallas_call(
        make_kernel(elem_start, nblocks, iface, halo is None),
        out_shape=jax.ShapeDtypeStruct((CTRL * channels, CTRL * CTRL), f32),
        scratch_shapes=scratch,
        cost_estimate=pl.CostEstimate(
            flops=4_000_000_000, transcendentals=0, bytes_accessed=4_000_000
        ),
        name="inner_elements" if halo is None else "outer_elements",
    )(*operands)


def exchange(block, axis, forward):
    return lax.ppermute(block, axis, forward)


def on_device(modes, connect, ghosts, inv_jacobian, young, density, ffd_cell, ffd_param, eigen):
    modes_n, nown = modes.shape[3], modes.shape[4]
    elems = connect.shape[3]
    iface = nown // 4
    n_slab, n_sub = lax.axis_size("slab"), lax.axis_size("sub")
    payload = pl.pallas_call(
        pack_kernel,
        out_shape=jax.ShapeDtypeStruct((ROWS, iface), jnp.float32),
        name="pack",
    )(modes, ffd_cell, ffd_param)
    ring = [(i, (i + 1) % n_slab) for i in range(n_slab)]
    back = [(target, source) for source, target in ring]
    block_id = ghosts // iface
    node_at = ghosts % iface
    if n_sub == 2:
        other = lax.ppermute(payload, "sub", [(0, 1), (1, 0)])
        both = jnp.stack([payload, other])
        below = lax.ppermute(both, "slab", ring)
        above = lax.ppermute(both, "slab", back)
        part_a = block_id // 3
        beside = (block_id % 3 != 1).astype(jnp.int32)
        place = jnp.where(part_a == 0, beside, jnp.where(part_a == 1, 2, 3 + beside))
        blocks, names = [below, other, above], ((0, 1), (None,), (0, 1))
    else:
        up = [(i, i + 1) for i in range(n_sub - 1)]
        down = [(target, source) for source, target in up]
        three = jnp.stack(
            [
                lax.ppermute(payload, "sub", up),
                payload,
                lax.ppermute(payload, "sub", down),
            ]
        )
        below = lax.ppermute(three, "slab", ring)
        above = lax.ppermute(three, "slab", back)
        place = block_id
        blocks, names = [below, three, above], ((0, 1, 2),) * 3
    arrays = (
        modes,
        ffd_cell,
        ffd_param,
        connect,
        inv_jacobian,
        young,
        density,
        eigen.reshape(modes_n, 1),
    )
    acc = run_elements(0, arrays, None, None)
    total = run_elements(
        elems // 2, arrays, (place * iface + node_at, blocks, names), acc
    )
    plane = CTRL * CTRL
    if n_slab == CTRL and n_sub == modes_n // GROUP == 2:
        block = total.reshape(CTRL, n_sub, 3 * GROUP, plane)
        return reduce_scatter(block, n_slab).reshape(3, GROUP, plane)
    groups = modes_n // GROUP
    design = (
        total.reshape(CTRL, groups, 3, GROUP, plane)
        .transpose(2, 1, 3, 0, 4)
        .reshape(3, modes_n, CTRL * plane)
    )
    by_cycle = lax.psum_scatter(design, "slab", scatter_dimension=2, tiled=True)
    return lax.psum_scatter(by_cycle, "sub", scatter_dimension=1, tiled=True)


def halve(block, dim, bit, axis, pairs):
    keep = lax.dynamic_index_in_dim(block, bit, dim, keepdims=False)
    send = lax.dynamic_index_in_dim(block, 1 - bit, dim, keepdims=False)
    return keep + lax.ppermute(send, axis, pairs)


def reduce_scatter(block, n_slab):
    place = lax.axis_index("slab")
    bits = n_slab.bit_length() - 1
    block = block.reshape((2,) * bits + block.shape[1:])

    def by_slab(value, power, dim):
        pairs = [(i, i ^ power) for i in range(n_slab)]
        return halve(value, dim, (place // power) % 2, "slab", pairs)

    block = by_slab(block, 1, bits - 1)
    block = halve(block, bits - 1, lax.axis_index("sub"), "sub", [(0, 1), (1, 0)])
    for level in range(1, bits):
        block = by_slab(block, 1 << level, bits - 1 - level)
    return block


def solution(mesh):
    return jax.shard_map(
        on_device,
        mesh=mesh,
        in_specs=(
            P("slab", "sub", None, None, None),
            P("slab", "sub", None, None),
            P("slab", "sub", None),
            P("slab", "sub", None, None, None, None),
            P("slab", "sub", None),
            P("slab", "sub", None),
            P("slab", "sub", None, None),
            P("slab", "sub", None, None),
            P(),
        ),
        out_specs=P(None, "sub", "slab"),
        check_vma=False,
    )
```

time: 226 us -> 75.9 us (0.34)
  waiting for transfers between devices: 77.6 us -> 19.7 us
  other arithmetic: 57.3 us -> 1.36 us
  local copies, waits for them, and re-layouts: 45.2 us -> 8.55 us
  Pallas kernels: 0 us -> 35.1 us
  matrix products: 18.4 us -> 0 us
  between operations: 13.6 us -> 0.16 us
    reduce_scatter x2 -> x0, waiting for transfers between devices: 66.6 us -> none  [the longest x1 55.3 us: on_device(): by_cycle = lax.psum_scatter(design, 'slab', scatter_dimension=2, tiled=True)]
    scatter-add x2 -> x0, other arithmetic: 41 us -> none  [assemble_step(): return (grad_acc.at[:, columns].add(contrib), None)]
    pallas_call x0 -> x3, Pallas kernels: none -> 35.1 us  [the longest x2 33.4 us: run_elements(): pl.pallas_call(make_kernel(elem_start, nblocks, iface, halo is None), out...]
    gather x5 -> x0, local copies, waits for them, and re-layouts: 22.9 us -> none  [the longest x4 19.3 us: assemble_step(): slot_vals[:, columns]]
    dot_general x11 -> x0, matrix products: 18.4 us -> none  [the longest x5 9.07 us: contract_step(): lax.dot_general(left, right, (((1,), (1,)), ((), ())), precision=lax.Prec...]
    mul x24 -> x0, other arithmetic: 12 us -> none  [the longest x6 5.77 us: element_block(): factor * (eshelby[comp_a][0] * jac[ref_dir][0] + eshelby[comp_a][1] * jac...]
    ppermute x4 -> x8, waiting for transfers between devices: 11 us -> 19.7 us  [the longest x5 19 us: halve(): return keep + lax.ppermute(send, axis, pairs)]
    slice x17 -> x0, local copies, waits for them, and re-layouts: 6.51 us -> none  [the longest x5 3.83 us: contract_step(): along_y = bernstein(cell_b[1], param_b[1], ctrl)]
  transfers between devices with their start and end apart: 6 -> 8, of which waited for: 5 -> 6; matrix products, arithmetic and copies ran while one was open for 1% -> 4% of each run, Pallas kernels for 0% -> 21%
where the time goes in v1:
time: 75.9 us; the launch traced here: 75.6 us
  Pallas kernels  35.1 us (46%)
  waiting for transfers between devices  19.7 us (26%)
  starting transfers between devices  10.7 us (14%)
  local copies, waits for them, and re-layouts  8.55 us (11%)
  other arithmetic  1.36 us (2%)
    pallas_call x2, Pallas kernels, run_elements(): pl.pallas_call(make_kernel(elem_start, nblocks, iface, halo is None), out...  33.4 us
    ppermute x5, waiting for transfers between devices, halve(): return keep + lax.ppermute(send, axis, pairs)  19 us
    unnamed x24, local copies, waits for them, and re-layouts  6.71 us
    ppermute x1, starting transfers between devices, on_device(): above = lax.ppermute(both, 'slab', back)  4.44 us
    ppermute x5, starting transfers between devices, halve(): return keep + lax.ppermute(send, axis, pairs)  3.33 us
    ppermute x1, starting transfers between devices, on_device(): other = lax.ppermute(payload, 'sub', [(0, 1), (1, 0)])  2.97 us
    pallas_call x1, Pallas kernels, on_device(): pl.pallas_call(pack_kernel, out_shape=jax.ShapeDtypeStruct((ROWS, iface),...  1.72 us
  transfers between devices with their start and end apart: 8, of which 6 were waited for; matrix products, arithmetic and copies ran while one was open for 4% of the time, Pallas kernels for 21%

profile of v1, /device:TPU:0, one launch (start us, length us, event | category | flops | bytes accessed | tf_op | source)
XLA Modules:
  0.0 75.6 jit_solution(925512588031470069)
XLA Ops:
  0.0 0.0 copy-start.5
  0.0 1.4 %copy.55.cells.refs_1_ = s32[1,1,3,2048]{3,2,1,0:T(4,128)} copy(s32[1,1,3,2048]{3,1,2,0:T(1,128)} %param.15) | data formatting | bytes 49152 | tf_op args[6]
  1.4 0.0 copy-done.5
  1.4 0.6 copy.56.params.refs_2_
  2.0 0.0 copy-start.4
  2.0 0.0 copy-start.2
  2.0 1.7 %pack.1 = f32[56,512]{1,0:T(8,128)} custom-call(f32[1,1,3,16,2048]{4,3,2,1,0:T(8,128)} %refs_0_.3, s32[1,1,3,2048]{3,2,1,0:T(4,128)} %copy.55.cells.refs_1_, f32[1,1,3,2048]{3,2,1,0:T(4,128)} %copy.56.params.refs_2_), custom_call_target="tpu_custom_call" | custom-call | tf_op jit(solution)/shard_map/pack/pallas_call | solution.py:395
  3.7 3.0 %collective-permute-start = (f32[56,512]{1,0:T(8,128)}, f32[56,512]{1,0:T(8,128)S(1)}, u32[]{:S(2)}, u32[]{:S(2)}) collective-permute-start(f32[56,512]{1,0:T(8,128)} %pack.1), channel_id=1, source_target_pairs={{0,1},{1,0},{2,3},{3,2},{4,5},{5,4},{6,7},{7,6},{8,9},{9,8},{10,11... | collective-permute-start | bytes 344072 | tf_op jit(solution)/shard_map/ppermute | solution.py:405
  6.7 0.0 copy-done.4
  6.7 0.6 copy.57.refs_3_
  7.3 0.0 copy-done.2
  7.3 0.0 copy-start.1
  7.3 0.7 copy.58.refs_4_
  8.1 0.0 copy-start.7
  8.1 0.7 copy-done.7
  8.7 0.7 copy.59.refs_7_
  9.4 0.7 collective-permute-done.refs_10_
  10.0 0.0 copy-start.3
  10.0 0.0 copy-done.1
  10.1 0.6 copy-done.3
  10.7 0.0 collective-permute-start.1
  10.7 4.4 %collective-permute-start.2 = (f32[2,56,512]{2,1,0:T(8,128)S(1)}, f32[2,56,512]{2,1,0:T(8,128)S(1)}, u32[]{:S(2)}, u32[]{:S(2)}) collective-permute-start(f32[2,56,512]{2,1,0:T(8,128)S(1)} %pad_maximum_fusion), channel_id=1, source_target_pairs={{2,0},{4,2},{6,4},{8,6},{10,8},{12,10},{14,12},{16,14},{18,16},{20... | collective-permute-start | bytes 688136 | tf_op jit(solution)/shard_map/ppermute | solution.py:408
  15.1 15.9 %inner_elements.1.refs_12_ = f32[768,256]{1,0:T(8,128)} custom-call(f32[1,1,3,16,2048]{4,3,2,1,0:T(8,128)} %refs_0_.3, s32[1,1,3,2048]{3,2,1,0:T(4,128)} %copy.55.cells.refs_1_, f32[1,1,3,2048]{3,2,1,0:T(4,128)} %copy.56.params.refs_2_, s32[1,1,27,256]{3,2,1,0:T(8,128)} %copy.57.refs_3_, f32[1,1,3,3,27,256]{5,4,3,2,1,0:T(8,128)} %copy.58.refs_4_, ...), custom_call_target="tpu_custom_call" | custom-call | flops 4000000000 | bytes 4000000 | tf_op jit(solution)/shard_map/inner_elements/pallas_call | solution.py:375
  31.0 0.0 copy-start.6
  31.0 0.7 copy-done.6
  31.7 0.6 fusion.1.refs_8_
  32.3 0.0 collective-permute-done.1.refs_9_
  32.3 0.0 copy-start.8
  32.3 0.0 collective-permute-done.2.refs_11_
  32.4 0.7 copy-done.8
  33.0 0.0 copy-start.9
  33.1 0.7 copy-done.9
  33.7 17.5 %outer_elements.1 = f32[768,256]{1,0:T(8,128)} custom-call(f32[1,1,3,16,2048]{4,3,2,1,0:T(8,128)} %refs_0_.3, s32[1,1,3,2048]{3,2,1,0:T(4,128)} %copy.55.cells.refs_1_, f32[1,1,3,2048]{3,2,1,0:T(4,128)} %copy.56.params.refs_2_, s32[1,1,27,256]{3,2,1,0:T(8,128)} %copy.57.refs_3_, f32[1,1,3,3,27,256]{5,4,3,2,1,0:T(8,128)} %copy.58.refs_4_, ...), custom_call_target="tpu_custom_call" | custom-call | flops 4000000000 | bytes 4000000 | tf_op jit(solution)/shard_map/outer_elements/pallas_call | solution.py:375
  51.3 0.0 copy-start
  51.3 1.1 %dynamic-slice_bitcast_fusion = f32[2,2,2,2,24,256]{5,4,3,2,1,0:T(8,128)S(1)} fusion(f32[2,2,2,2,2,24,256]{6,5,4,3,2,1,0:T(8,128)} %bitcast.32, s32[]{:T(128)S(6)} %select_n.98), kind=kLoop, calls=%fused_computation.1 | loop fusion | bytes 786436 | tf_op jit(solution)/shard_map/jit(dynamic_index_in_dim)/squeeze | solution.py:457
  52.4 0.1 collective-permute-start.3
  52.5 1.7 %collective-permute-done.3 = f32[2,2,2,2,24,256]{5,4,3,2,1,0:T(8,128)S(1)} collective-permute-done((f32[2,2,2,2,24,256]{5,4,3,2,1,0:T(8,128)S(1)}, f32[2,2,2,2,24,256]{5,4,3,2,1,0:T(8,128)S(1)}, u32[]{:S(2)}, u32[]{:S(2)}) %collective-permute-start.3) | collective-permute-done | bytes 393248 | tf_op jit(solution)/shard_map/ppermute | solution.py:458
  54.2 0.0 copy-done
  54.2 0.1 bitcast_add_fusion
  54.3 1.8 %collective-permute-start.4 = (f32[2,2,2,24,256]{4,3,2,1,0:T(8,128)S(1)}, f32[2,2,2,24,256]{4,3,2,1,0:T(8,128)S(1)}, u32[]{:S(2)}, u32[]{:S(2)}) collective-permute-start(f32[2,2,2,24,256]{4,3,2,1,0:T(8,128)S(1)} %dynamic-slice_bitcast_fusion.1), channel_id=1, source_target_pairs={{0,1},{1,0},{2,3},{3,2},{4,5},{5,4},{6,7},{7,6},{8,9},{9,8},{10,11... | collective-permute-start | bytes 589832 | tf_op jit(solution)/shard_map/ppermute | solution.py:458
  56.0 5.2 %collective-permute-done.4 = f32[2,2,2,24,256]{4,3,2,1,0:T(8,128)S(1)} collective-permute-done((f32[2,2,2,24,256]{4,3,2,1,0:T(8,128)S(1)}, f32[2,2,2,24,256]{4,3,2,1,0:T(8,128)S(1)}, u32[]{:S(2)}, u32[]{:S(2)}) %collective-permute-start.4) | collective-permute-done | bytes 196640 | tf_op jit(solution)/shard_map/ppermute | solution.py:458
  61.3 0.1 collective-permute-start.5
  61.4 4.6 %collective-permute-done.5 = f32[2,2,24,256]{3,2,1,0:T(8,128)S(1)} collective-permute-done((f32[2,2,24,256]{3,2,1,0:T(8,128)S(1)}, f32[2,2,24,256]{3,2,1,0:T(8,128)S(1)}, u32[]{:S(2)}, u32[]{:S(2)}) %collective-permute-start.5) | collective-permute-done | bytes 98336 | tf_op jit(solution)/shard_map/ppermute | solution.py:458
  66.0 0.1 collective-permute-start.6
  66.2 4.0 %collective-permute-done.6 = f32[2,24,256]{2,1,0:T(8,128)S(1)} collective-permute-done((f32[2,24,256]{2,1,0:T(8,128)S(1)}, f32[2,24,256]{2,1,0:T(8,128)S(1)}, u32[]{:S(2)}, u32[]{:S(2)}) %collective-permute-start.6) | collective-permute-done | bytes 49184 | tf_op jit(solution)/shard_map/ppermute | solution.py:458
  70.2 1.3 %collective-permute-start.7 = (f32[24,256]{1,0:T(8,128)S(1)}, f32[24,256]{1,0:T(8,128)S(1)}, u32[]{:S(2)}, u32[]{:S(2)}) collective-permute-start(f32[24,256]{1,0:T(8,128)S(1)} %dynamic-slice_bitcast_fusion.4), channel_id=1, source_target_pairs={{0,16},{2,18},{4,20},{6,22},{8,24},{10,26},{12,28},{14,30},{16,0},... | collective-permute-start | bytes 73736 | tf_op jit(solution)/shard_map/ppermute | solution.py:458
  71.5 3.5 %collective-permute-done.7 = f32[24,256]{1,0:T(8,128)S(1)} collective-permute-done((f32[24,256]{1,0:T(8,128)S(1)}, f32[24,256]{1,0:T(8,128)S(1)}, u32[]{:S(2)}, u32[]{:S(2)}) %collective-permute-start.7) | collective-permute-done | bytes 24608 | tf_op jit(solution)/shard_map/ppermute | solution.py:458
  75.0 0.6 fusion
  (8 shorter events, 0.1 us)
Async XLA Ops:
  0.0 1.4 %copy-start.5 = (f32[1,1,3,2048]{3,1,2,0:T(1,128)S(1)}, f32[1,1,3,2048]{3,1,2,0:T(1,128)}, u32[]{:S(2)}) copy-start(f32[1,1,3,2048]{3,1,2,0:T(1,128)} %param.16) | copy-start | bytes 73732
  2.0 4.7 %copy-start.4 = (s32[1,1,27,256]{3,1,2,0:T(1,128)S(1)}, s32[1,1,27,256]{3,1,2,0:T(1,128)}, u32[]{:S(2)}) copy-start(s32[1,1,27,256]{3,1,2,0:T(1,128)} %param.10) | copy-start | bytes 82948
  2.0 5.3 %copy-start.2 = (f32[1,1,3,3,27,256]{5,1,4,3,2,0:T(1,128)S(1)}, f32[1,1,3,3,27,256]{5,1,4,3,2,0:T(1,128)}, u32[]{:S(2)}) copy-start(f32[1,1,3,3,27,256]{5,1,4,3,2,0:T(1,128)} %param.12) | copy-start | bytes 746500
  3.7 6.3 %collective-permute-start = (f32[56,512]{1,0:T(8,128)}, f32[56,512]{1,0:T(8,128)S(1)}, u32[]{:S(2)}, u32[]{:S(2)}) collective-permute-start(f32[56,512]{1,0:T(8,128)} %pack.1), channel_id=1, source_target_pairs={{0,1},{1,0},{2,3},{3,2},{4,5},{5,4},{6,7},{7,6},{8,9},{9,8},{10,11... | collective-permute-start | bytes 344072 | tf_op jit(solution)/shard_map/ppermute | solution.py:405
  7.3 2.7 %copy-start.1 = (f32[56,512]{1,0:T(8,128)S(1)}, f32[56,512]{1,0:T(8,128)}, u32[]{:S(2)}) copy-start(f32[56,512]{1,0:T(8,128)} %pack.1) | copy-start | bytes 344068
  8.1 0.7 copy-start.7
  10.0 0.6 copy-start.3
  10.7 21.7 %collective-permute-start.1 = (f32[2,56,512]{2,1,0:T(8,128)S(1)}, f32[2,56,512]{2,1,0:T(8,128)S(1)}, u32[]{:S(2)}, u32[]{:S(2)}) collective-permute-start(f32[2,56,512]{2,1,0:T(8,128)S(1)} %pad_maximum_fusion), channel_id=1, source_target_pairs={{0,2},{2,4},{4,6},{6,8},{8,10},{10,12},{12,14},{14,16},{16,18},{18... | collective-permute-start | bytes 688136 | tf_op jit(solution)/shard_map/ppermute | solution.py:407
  10.7 21.7 %collective-permute-start.2 = (f32[2,56,512]{2,1,0:T(8,128)S(1)}, f32[2,56,512]{2,1,0:T(8,128)S(1)}, u32[]{:S(2)}, u32[]{:S(2)}) collective-permute-start(f32[2,56,512]{2,1,0:T(8,128)S(1)} %pad_maximum_fusion), channel_id=1, source_target_pairs={{2,0},{4,2},{6,4},{8,6},{10,8},{12,10},{14,12},{16,14},{18,16},{20... | collective-permute-start | bytes 688136 | tf_op jit(solution)/shard_map/ppermute | solution.py:408
  31.0 0.7 copy-start.6
  32.3 0.7 copy-start.8
  33.0 0.7 copy-start.9
  51.3 2.9 %copy-start = (f32[768,256]{1,0:T(8,128)S(1)}, f32[768,256]{1,0:T(8,128)}, u32[]{:S(2)}) copy-start(f32[768,256]{1,0:T(8,128)} %outer_elements.1) | copy-start | bytes 2359300
  52.4 1.8 %collective-permute-start.3 = (f32[2,2,2,2,24,256]{5,4,3,2,1,0:T(8,128)S(1)}, f32[2,2,2,2,24,256]{5,4,3,2,1,0:T(8,128)S(1)}, u32[]{:S(2)}, u32[]{:S(2)}) collective-permute-start(f32[2,2,2,2,24,256]{5,4,3,2,1,0:T(8,128)S(1)} %dynamic-slice_bitcast_fusion), channel_id=1, source_target_pairs={{0,2},{2,0},{4,6},{6,4},{8,10},{10,8},{12,14},{14,12},{16,18},{18,... | collective-permute-start | bytes 1179656 | tf_op jit(solution)/shard_map/ppermute | solution.py:458
  54.3 7.0 %collective-permute-start.4 = (f32[2,2,2,24,256]{4,3,2,1,0:T(8,128)S(1)}, f32[2,2,2,24,256]{4,3,2,1,0:T(8,128)S(1)}, u32[]{:S(2)}, u32[]{:S(2)}) collective-permute-start(f32[2,2,2,24,256]{4,3,2,1,0:T(8,128)S(1)} %dynamic-slice_bitcast_fusion.1), channel_id=1, source_target_pairs={{0,1},{1,0},{2,3},{3,2},{4,5},{5,4},{6,7},{7,6},{8,9},{9,8},{10,11... | collective-permute-start | bytes 589832 | tf_op jit(solution)/shard_map/ppermute | solution.py:458
  61.3 4.7 %collective-permute-start.5 = (f32[2,2,24,256]{3,2,1,0:T(8,128)S(1)}, f32[2,2,24,256]{3,2,1,0:T(8,128)S(1)}, u32[]{:S(2)}, u32[]{:S(2)}) collective-permute-start(f32[2,2,24,256]{3,2,1,0:T(8,128)S(1)} %dynamic-slice_bitcast_fusion.2), channel_id=1, source_target_pairs={{0,4},{2,6},{4,0},{6,2},{8,12},{10,14},{12,8},{14,10},{16,20},{18,... | collective-permute-start | bytes 294920 | tf_op jit(solution)/shard_map/ppermute | solution.py:458
  66.0 4.2 %collective-permute-start.6 = (f32[2,24,256]{2,1,0:T(8,128)S(1)}, f32[2,24,256]{2,1,0:T(8,128)S(1)}, u32[]{:S(2)}, u32[]{:S(2)}) collective-permute-start(f32[2,24,256]{2,1,0:T(8,128)S(1)} %dynamic-slice_bitcast_fusion.3), channel_id=1, source_target_pairs={{0,8},{2,10},{4,12},{6,14},{8,0},{10,2},{12,4},{14,6},{16,24},{18,... | collective-permute-start | bytes 147464 | tf_op jit(solution)/shard_map/ppermute | solution.py:458
  70.2 4.8 %collective-permute-start.7 = (f32[24,256]{1,0:T(8,128)S(1)}, f32[24,256]{1,0:T(8,128)S(1)}, u32[]{:S(2)}, u32[]{:S(2)}) collective-permute-start(f32[24,256]{1,0:T(8,128)S(1)} %dynamic-slice_bitcast_fusion.4), channel_id=1, source_target_pairs={{0,16},{2,18},{4,20},{6,22},{8,24},{10,26},{12,28},{14,30},{16,0},... | collective-permute-start | bytes 73736 | tf_op jit(solution)/shard_map/ppermute | solution.py:458
